TPU v7x, 32 devices: a whole 2x2x4 slice. The times are simulated.
32 devices in a mesh: zero: 8 (over y, x, core), cols: 4 (over z).
Axes of the slice: x: 2, y: 2, z: 4, core: 2. Of those that a mesh axis runs over, the one named last changes fastest.
Arguments:
- train_gate: bfloat16 [4096, 11008], P('zero', 'cols'), may hold values from -0.125 to 0.125
- low_gate: bfloat16 [4096, 64], P('zero'), may hold values from -0.09375 to 0.09375
- high_gate: bfloat16 [64, 11008], P(None, 'cols'), may hold values from -0.75 to 0.75
- train_up: bfloat16 [4096, 11008], P('zero', 'cols'), may hold values from -0.125 to 0.125
- low_up: bfloat16 [4096, 64], P('zero'), may hold values from -0.09375 to 0.09375
- high_up: bfloat16 [64, 11008], P(None, 'cols'), may hold values from -0.75 to 0.75
- norm_train: float32 [4096], P(('zero', 'cols')), may hold values from 0.25 to 1.75
- norm_step: float32 [4096], P(('zero', 'cols')), may hold values from -0.3 to 0.3
Outputs:
- ready_gate: bfloat16 [4096, 11008], P(None, 'cols')
- ready_up: bfloat16 [4096, 11008], P(None, 'cols')
- factor_gate: float32 [11008], P('cols')
- factor_up: float32 [11008], P('cols')
- serve_norm: bfloat16 [4096], replicated
All inputs are finite; a program needn't handle non-finite values. Where the computation divides by a largest or mean magnitude, that divisor is 1e-20 or more.
Results may differ from a plain program's by a relative error of at most 0.001.
Values may be sent and summed in bfloat16 or wider, within the bound.
A program may use at most 192 MiB of HBM per device.

v0:
```python
import jax
import jax.numpy as jnp
from jax import lax
from jax.sharding import PartitionSpec as P

D_MODEL = 4096


mix_rate = 1.0


def shards(train_gate, low_gate, high_gate, train_up, low_up, high_up, norm_train, norm_step):
    latest_gate = train_gate.astype(jnp.float32) + mix_rate * jnp.dot(
        low_gate, high_gate, preferred_element_type=jnp.float32
    )
    latest_up = train_up.astype(jnp.float32) + mix_rate * jnp.dot(
        low_up, high_up, preferred_element_type=jnp.float32
    )
    total_gate, total_up = lax.psum(
        (jnp.sum(jnp.abs(latest_gate), axis=0), jnp.sum(jnp.abs(latest_up), axis=0)), "zero"
    )
    factor_gate = total_gate / D_MODEL
    factor_up = total_up / D_MODEL
    narrow_gate, narrow_up = (
        (latest_gate / factor_gate).astype(jnp.bfloat16),
        (latest_up / factor_up).astype(jnp.bfloat16),
    )
    ready_gate, ready_up = (
        lax.all_gather(narrow_gate, "zero", axis=0, tiled=True),
        lax.all_gather(narrow_up, "zero", axis=0, tiled=True),
    )
    serve_norm = lax.all_gather(
        (norm_train + norm_step).astype(jnp.bfloat16), ("zero", "cols"), axis=0, tiled=True
    )
    return (ready_gate, ready_up, factor_gate, factor_up, serve_norm)


def solution(mesh):
    return jax.shard_map(
        shards,
        mesh=mesh,
        in_specs=(
            P("zero", "cols"),
            P("zero", None),
            P(None, "cols"),
            P("zero", "cols"),
            P("zero", None),
            P(None, "cols"),
            P(("zero", "cols")),
            P(("zero", "cols")),
        ),
        out_specs=(P(None, "cols"), P(None, "cols"), P("cols"), P("cols"), P()),
        check_vma=False,
    )
```

profile of v0, /device:TPU:0, one launch (start us, length us, event | category | flops | bytes accessed | tf_op | source)
XLA Modules:
  0.0 323.6 jit_solution(7522673026313851749)
XLA Ops:
  7.2 0.0 copy-start
  7.2 0.0 copy-start.3
  7.2 0.0 copy-start.4
  7.2 0.0 all-gather.6.cloned.1.call-start
  7.2 0.9 copy-done
  8.2 0.0 copy-start.5
  8.2 5.4 %abs_reduce_fusion.1 = (f32[2752]{0:T(1024)S(1)}, f32[512,2752]{0,1:T(8,128)}) fusion(bf16[512,64]{0,1:T(8,128)(2,1)} %param.9, bf16[64,2752]{1,0:T(8,128)(2,1)S(1)} %copy-done, bf16[512,2752]{0,1:T(8,128)(2,1)} %param.8), kind=kOutput, calls=%fused_computation.4 | convolution fusion | flops 185988416 | bytes 8882944 | tf_op jit(solution)/shard_map/dot_general | solution.py:13
  13.6 0.0 copy-done.3
  13.6 0.0 copy-done.4
  13.6 0.0 copy-done.5
  13.6 3.5 %abs_reduce_fusion = (f32[2752]{0:T(1024)S(1)}, f32[512,2752]{0,1:T(8,128)}) fusion(bf16[512,64]{0,1:T(8,128)(2,1)S(1)} %copy-done.5, bf16[64,2752]{1,0:T(8,128)(2,1)S(1)} %copy-done.4, bf16[512,2752]{0,1:T(8,128)(2,1)S(1)} %copy-done.3), kind=kOutput, calls=%fused_computation.1 | convolution fusion | flops 185988416 | bytes 8882944 | tf_op jit(solution)/shard_map/dot_general | solution.py:16
  17.2 25.5 %all-reduce = (f32[2752]{0:T(1024)S(1)}, f32[2752]{0:T(1024)S(1)}) all-reduce(f32[2752]{0:T(1024)S(1)} %get-tuple-element.7, f32[2752]{0:T(1024)S(1)} %get-tuple-element.9), channel_id=1, replica_groups=mesh['zero'=8,'cols'=4] {'zero'}, use_global_device_ids=true, to_apply=%region_1.0 | all-reduce | flops 5504 | bytes 44032 | tf_op jit(solution)/shard_map/psum | solution.py:19
  42.7 0.0 copy-start.6
  42.7 4.4 %divide_convert_fusion = bf16[512,2752]{0,1:T(8,128)(2,1)} fusion(f32[512,2752]{0,1:T(8,128)} %get-tuple-element.10, f32[2752]{0:T(1024)S(1)} %broadcast_multiply_fusion), kind=kLoop, calls=%fused_computation | loop fusion | flops 2818048 | bytes 8465152 | tf_op jit(solution)/shard_map/convert_element_type | solution.py:26
  47.1 0.0 all-gather.6.cloned.1.call-update
  47.2 0.0 copy-done.6
  47.2 0.0 all-gather.4.cloned.1.call-start
  47.2 0.0 copy-start.7
  47.2 0.0 copy-start.8
  47.2 0.0 copy-start.9
  47.3 4.4 %divide_convert_fusion.1 = bf16[512,2752]{0,1:T(8,128)(2,1)} fusion(f32[512,2752]{0,1:T(8,128)} %get-tuple-element.8, f32[2752]{0:T(1024)S(1)} %broadcast_multiply_fusion.1), kind=kLoop, calls=%fused_computation.3 | loop fusion | flops 2818048 | bytes 8465152 | tf_op jit(solution)/shard_map/convert_element_type | solution.py:25
  51.6 0.0 all-gather.4.cloned.1.call-update
  51.7 0.0 copy-done.7
  51.7 0.0 copy-done.8
  51.7 0.0 copy-done.9
  51.7 66.0 %all-gather = bf16[32,1,128]{2,1,0:T(2,128)(2,1)S(1)} all-gather(bf16[1,1,128]{2,1,0:T(2,128)(2,1)S(1)} %convert_bitcast_fusion), channel_id=1, replica_groups=mesh['zero'=8,'cols'=4] {'zero','cols'}, dimensions={0}, use_global_device_ids=true | all-gather | bytes 8448 | tf_op jit(solution)/shard_map/all_gather | solution.py:32
  117.7 0.6 reduce
  118.3 47.0 %all-gather.6.cloned.1.call-done = bf16[4096,2752]{0,1:T(8,128)(2,1)} async-done(((bf16[512,2752]{0,1:T(8,128)(2,1)}), bf16[4096,2752]{0,1:T(8,128)(2,1)}) %all-gather.6.cloned.1.call-update) | async-done | bytes 22544400 | tf_op jit(solution)/shard_map/all_gather | solution.py:30
  165.3 121.0 %all-gather.4.cloned.1.call-done = bf16[4096,2752]{0,1:T(8,128)(2,1)} async-done(((bf16[512,2752]{0,1:T(8,128)(2,1)}), bf16[4096,2752]{0,1:T(8,128)(2,1)}) %all-gather.4.cloned.1.call-update) | async-done | bytes 22544400 | tf_op jit(solution)/shard_map/all_gather | solution.py:29
  286.3 0.0 copy-start.2
  286.4 21.1 %copy.15 = bf16[4096,2752]{0,1:T(8,128)(2,1)} copy(bf16[4096,2752]{0,1:T(8,128)(2,1)} %all-gather.4.cloned.1.call-done) | data formatting | bytes 45088768
  307.5 1.2 copy-done.2
  308.7 0.0 copy-start.1
  308.7 8.1 %copy.16 = bf16[4096,2752]{0,1:T(8,128)(2,1)} copy(bf16[4096,2752]{0,1:T(8,128)(2,1)S(1)} %copy-done.2) | data formatting | bytes 45088768
  316.7 0.0 copy-done.1
  (3 shorter events, 0.0 us)
Async XLA Ops:
  7.2 1.0 copy-start
  7.2 6.4 %copy-start.3 = (bf16[512,2752]{0,1:T(8,128)(2,1)S(1)}, bf16[512,2752]{0,1:T(8,128)(2,1)}, u32[]{:S(2)}) copy-start(bf16[512,2752]{0,1:T(8,128)(2,1)} %param.11) | copy-start | bytes 8454148
  7.2 6.4 %copy-start.4 = (bf16[64,2752]{1,0:T(8,128)(2,1)S(1)}, bf16[64,2752]{1,0:T(8,128)(2,1)}, u32[]{:S(2)}) copy-start(bf16[64,2752]{1,0:T(8,128)(2,1)} %param.13) | copy-start | bytes 1056772
  7.2 158.1 %all-gather.6.cloned.1.call-start = ((), (), s32[]{:S(2)}) async-start(), calls=%async_computation.1 | async-start | bytes 25362432 | tf_op jit(solution)/shard_map/all_gather | solution.py:30
  8.2 5.5 %copy-start.5 = (bf16[512,64]{0,1:T(8,128)(2,1)S(1)}, bf16[512,64]{0,1:T(8,128)(2,1)}, u32[]{:S(2)}) copy-start(bf16[512,64]{0,1:T(8,128)(2,1)} %param.12) | copy-start | bytes 196612
  42.7 4.4 %copy-start.6 = (f32[2752]{0:T(1024)}, f32[2752]{0:T(1024)S(1)}, u32[]{:S(2)}) copy-start(f32[2752]{0:T(1024)S(1)} %broadcast_multiply_fusion) | copy-start | bytes 33028
  47.2 239.2 %all-gather.4.cloned.1.call-start = ((), (), s32[]{:S(2)}) async-start(), calls=%async_computation | async-start | bytes 25362432 | tf_op jit(solution)/shard_map/all_gather | solution.py:29
  47.2 4.4 %copy-start.7 = (f32[2752]{0:T(1024)}, f32[2752]{0:T(1024)S(1)}, u32[]{:S(2)}) copy-start(f32[2752]{0:T(1024)S(1)} %broadcast_multiply_fusion.1) | copy-start | bytes 33028
  47.2 4.4 %copy-start.8 = (f32[128]{0:T(128)S(1)}, f32[128]{0:T(128)}, u32[]{:S(2)}) copy-start(f32[128]{0:T(128)} %param.14) | copy-start | bytes 1540
  47.2 4.4 %copy-start.9 = (f32[128]{0:T(128)S(1)}, f32[128]{0:T(128)}, u32[]{:S(2)}) copy-start(f32[128]{0:T(128)} %param.15) | copy-start | bytes 1540
  286.3 22.3 %copy-start.2 = (bf16[4096,2752]{0,1:T(8,128)(2,1)S(1)}, bf16[4096,2752]{0,1:T(8,128)(2,1)}, u32[]{:S(2)}) copy-start(bf16[4096,2752]{0,1:T(8,128)(2,1)} %all-gather.6.cloned.1.call-done) | copy-start | bytes 67633152
  308.7 8.1 %copy-start.1 = (bf16[64,2752]{1,0:T(8,128)(2,1)S(1)}, bf16[64,2752]{1,0:T(8,128)(2,1)}, u32[]{:S(2)}) copy-start(bf16[64,2752]{1,0:T(8,128)(2,1)} %param.10) | copy-start | bytes 1056772
Sparse Core Ops, SparseCore 0:
  47.3 117.9 all-gather.5
  167.8 118.5 all-gather.3
where the time goes:
time: 324 us
  waiting for transfers between devices  168 us (52%)
  blocking collectives  91.5 us (28%)
  local copies, waits for them, and re-layouts  31.3 us (10%)
  between operations  14.1 us (4%)
  other arithmetic  9.46 us (3%)
  matrix products  8.98 us (3%)
    all_gather x1, waiting for transfers between devices, shards(): lax.all_gather(narrow_gate, 'zero', axis=0, tiled=True)  121 us
    all_gather x1, blocking collectives, shards(): lax.all_gather((norm_train + norm_step).astype(jnp.bfloat16), ('zero', 'c...  66 us
    all_gather x1, waiting for transfers between devices, shards(): lax.all_gather(narrow_up, 'zero', axis=0, tiled=True)  47 us
    unnamed x22, local copies, waits for them, and re-layouts  31.3 us
    psum x1, blocking collectives, shards(): lax.psum((jnp.sum(jnp.abs(latest_gate), axis=0), jnp.sum(jnp.abs(latest_u...  25.5 us
  transfers between devices with their start and end apart: 2, of which 2 were waited for; matrix products, arithmetic and copies ran while one was open for 2% of the time, Pallas kernels for 0%

commit v1 on v0

v1 whole, which is shorter than its diff:
```python
import functools

import jax
import jax.numpy as jnp
from jax import lax
from jax.experimental import pallas as pl
from jax.experimental.pallas import tpu as pltpu
from jax.sharding import PartitionSpec as P

mix_rate = 1.0
CHUNKS = 4
WINDOW = 4
LANES = 128
TILE = 16
BLOCK = 704
MESH = pl.DeviceIdType.MESH

OWN_X, OWN_Y, OWN_S, DIAG, X_S, Y_S, D_S = range(7)


def one_half(low, i):
    rank = low.shape[0] // 2
    mine, none = low[i * rank:(i + 1) * rank], jnp.zeros((rank, low.shape[1]), low.dtype)
    return jnp.concatenate([none, mine] if i else [mine, none], axis=0)


def gather_kernel(
    n, cols, axes,
    gate, up, low, high, norm,
    all_gate, all_up, all_low, total, scale, all_norm,
    own_gate, own_up, own_low, vhigh, part, landed,
    send, recv, local_sem, sum_send, sum_recv, norm_send, norm_recv, z_send, z_recv,
):
    zero_axis, cols_axis = axes
    me, col = lax.axis_index(zero_axis), lax.axis_index(cols_axis)
    core, x, y = me % 2, (me // 2) % 2, me // 4
    to_s, to_x, to_y = 1 - 2 * core, 2 - 4 * x, 4 - 8 * y
    sib, xn, yn = me + to_s, me + to_x, me + to_y
    diag = xn + to_y
    width = gate.shape[0]
    d_model = n * gate.shape[1]

    barrier = pltpu.get_barrier_semaphore()
    for peer in (sib, xn, yn):
        pl.semaphore_signal(barrier, inc=1, device_id={zero_axis: peer, cols_axis: col}, device_id_type=MESH)
    for step in range(1, cols):
        pl.semaphore_signal(
            barrier, inc=1, device_id={zero_axis: me, cols_axis: (col + step) % cols}, device_id_type=MESH
        )
    pl.semaphore_wait(barrier, 3 + cols - 1)

    size = width // CHUNKS
    half = low.shape[0] // 2
    pieces = [(low, all_low, 0, half), (low, all_low, half, half)]
    for k in range(CHUNKS):
        pieces += [(gate, all_gate, k * size, size), (up, all_up, k * size, size)]
    count = len(pieces)

    def place(p, owner):
        _, out, start, length = pieces[p]
        return out.at[owner, pl.ds(start, length)]

    def own(p):
        ref, _, start, length = pieces[p]
        return ref.at[pl.ds(start, length)]

    def copy(kind, p, src, owner, target):
        return pltpu.make_async_remote_copy(
            src_ref=src,
            dst_ref=place(p, owner),
            send_sem=send.at[kind, p],
            recv_sem=recv.at[kind, p],
            device_id={zero_axis: target, cols_axis: col},
            device_id_type=MESH,
        )

    started = []

    def go(c):
        c.start()
        started.append(c)

    def send_own(p):
        go(copy(OWN_X, p, own(p), me, xn))
        go(copy(OWN_Y, p, own(p), me, yn))
        go(copy(OWN_S, p, own(p), me, sib))

    for p in range(WINDOW):
        send_own(p)

    def z_copy(step):
        return pltpu.make_async_remote_copy(
            src_ref=norm,
            dst_ref=all_norm.at[me, col],
            send_sem=z_send.at[step],
            recv_sem=z_recv.at[step],
            device_id={zero_axis: me, cols_axis: (col + step) % cols},
            device_id_type=MESH,
        )

    for step in range(1, cols):
        go(z_copy(step))
    keep_norm = pltpu.make_async_copy(norm, all_norm.at[me, col], local_sem.at[0])
    keep_norm.start()

    loads = [
        pltpu.make_async_copy(src, dst, local_sem.at[1 + i])
        for i, (src, dst) in enumerate(((gate, own_gate), (up, own_up), (low, own_low), (high, vhigh)))
    ]
    for load in loads:
        load.start()
    for load in loads:
        load.wait()
    stores = [
        pltpu.make_async_copy(src, dst.at[me], local_sem.at[5 + i])
        for i, (src, dst) in enumerate(((own_gate, all_gate), (own_up, all_up), (own_low, all_low)))
    ]
    for store in stores:
        store.start()

    full, rest = divmod(width, LANES)

    def each_block(body):
        def step(t, carry):
            body(t, pl.multiple_of(t * LANES, LANES))
            return carry

        lax.fori_loop(0, full, step, 0)
        if rest:
            body(full, width - LANES)

    for i, shard in enumerate((own_gate, own_up)):
        lower = one_half(own_low, i)

        def add(t, start, shard=shard, lower=lower, i=i):
            at = pl.ds(start, LANES)
            size = jnp.abs(shard[at].astype(jnp.float32) + mix_rate * jnp.dot(
                vhigh[at], lower, preferred_element_type=jnp.float32
            ))
            lanes = sum(size[:, k:k + LANES] for k in range(0, shard.shape[1], LANES))
            part[0, i, pl.ds(t, 1)] = jnp.sum(lanes.T, axis=0, keepdims=True)

        each_block(add)
    keep_norm.wait()

    def exchange(stage, peer):
        held = 1 << stage
        at = pl.ds((me // held) * held, held)
        target = {zero_axis: peer, cols_axis: col}
        go(pltpu.make_async_remote_copy(
            src_ref=part.at[stage], dst_ref=landed.at[stage], send_sem=sum_send.at[stage],
            recv_sem=sum_recv.at[stage], device_id=target, device_id_type=MESH,
        ))
        go(pltpu.make_async_remote_copy(
            src_ref=all_norm.at[at], dst_ref=all_norm.at[at], send_sem=norm_send.at[stage],
            recv_sem=norm_recv.at[stage], device_id=target, device_id_type=MESH,
        ))

    def finish(stage, peer):
        held = 1 << stage
        at = pl.ds((peer // held) * held, held)
        pltpu.make_async_copy(landed.at[stage], landed.at[stage], sum_recv.at[stage]).wait()
        pltpu.make_async_copy(all_norm.at[at], all_norm.at[at], norm_recv.at[stage]).wait()
        summed = part[stage] + landed[stage]
        if stage < 2:
            part[stage + 1] = summed
            return
        total[...] = summed
        for i in range(2):
            def spread(t, start, i=i):
                row = jnp.broadcast_to(total[i, pl.ds(t, 1)], (LANES, LANES))
                scale[i, pl.ds(start, LANES)] = 1.0 / (row.T / d_model)

            each_block(spread)

    def arrived(kind, p, owner):
        here = place(p, owner)
        pltpu.make_async_copy(here, here, recv.at[kind, p]).wait()

    def diag_arrived(p):
        arrived(DIAG, p, diag)
        go(copy(D_S, p, place(p, diag), diag, sib))

    for p in range(count):
        arrived(OWN_X, p, xn)
        if p + WINDOW < count:
            send_own(p + WINDOW)
        if p % 2 == 0:
            go(copy(DIAG, p, place(p, xn), xn, yn))
        go(copy(X_S, p, place(p, xn), xn, sib))
        arrived(OWN_Y, p, yn)
        if p % 2 == 1:
            go(copy(DIAG, p, place(p, yn), yn, xn))
        go(copy(Y_S, p, place(p, yn), yn, sib))
        if p == 1:
            for step in range(1, cols):
                back = all_norm.at[me, (col + cols - step) % cols]
                pltpu.make_async_copy(back, back, z_recv.at[step]).wait()
            exchange(0, sib)
        if p == 3:
            finish(0, sib)
        if p == 4:
            exchange(1, xn)
        if p == count - 3:
            finish(1, xn)
        if p == count - 2:
            exchange(2, yn)
    for p in range(count - 1):
        diag_arrived(p)
    finish(2, yn)
    diag_arrived(count - 1)
    for p in range(count):
        arrived(OWN_S, p, sib)
        arrived(X_S, p, sib + to_x)
        arrived(Y_S, p, sib + to_y)
        arrived(D_S, p, sib + to_x + to_y)
    for store in stores:
        store.wait()
    for c in started:
        c.wait_send()


def merge_kernel(gate, up, low, high, scale, out_gate, out_up):
    lanes = gate.shape[1]
    for i, (shard, out) in enumerate(((gate, out_gate), (up, out_up))):
        lower = one_half(low, i)

        latest = shard[...].astype(jnp.float32) + mix_rate * jnp.dot(
            high[...], lower, preferred_element_type=jnp.float32
        )
        by = scale[i]
        for k in range(0, lanes, LANES):
            out[:, k:k + LANES] = (latest[:, k:k + LANES] * by).astype(out.dtype)


def merge(all_gate, all_up, all_low, high, scale):
    n, width, lanes = all_gate.shape
    block = next(width // c for c in range(1, width) if width % (c * TILE) == 0 and width // c <= BLOCK)
    shard = pl.BlockSpec((None, block, lanes), lambda r, b: (b, r, 0))
    out = pl.BlockSpec((block, lanes), lambda r, b: (r, b))
    return pl.pallas_call(
        merge_kernel,
        grid=(width // block, n),
        in_specs=[
            shard,
            shard,
            pl.BlockSpec((None,) + all_low.shape[1:], lambda r, b: (b, 0, 0)),
            pl.BlockSpec((block, high.shape[1]), lambda r, b: (r, 0)),
            pl.BlockSpec((2, block, LANES), lambda r, b: (0, r, 0)),
        ],
        out_specs=[out, out],
        out_shape=[jax.ShapeDtypeStruct((width, n * lanes), jnp.bfloat16)] * 2,
        compiler_params=pltpu.CompilerParams(vmem_limit_bytes=40 * 1024 * 1024),
    )(all_gate, all_up, all_low, high, scale)


def gathered(mesh, gate, up, low, high, stepped):
    n, cols = mesh.shape["zero"], mesh.shape["cols"]
    width, lanes = gate.shape
    piece = jnp.broadcast_to(stepped[None, :], (8, stepped.shape[0]))
    count = 2 * CHUNKS + 2
    lines = pl.cdiv(width, LANES)
    anywhere = pl.BlockSpec(memory_space=pl.ANY)
    vmem = pl.BlockSpec(memory_space=pltpu.VMEM)
    dma = lambda *shape: pltpu.SemaphoreType.DMA(shape)
    return pl.pallas_call(
        functools.partial(gather_kernel, n, cols, ("zero", "cols")),
        in_specs=[anywhere] * 4 + [vmem],
        out_specs=[anywhere] * 3 + [vmem] * 3,
        out_shape=[
            jax.ShapeDtypeStruct((n,) + gate.shape, jnp.bfloat16),
            jax.ShapeDtypeStruct((n,) + gate.shape, jnp.bfloat16),
            jax.ShapeDtypeStruct((n,) + low.shape, jnp.bfloat16),
            jax.ShapeDtypeStruct((2, lines, LANES), jnp.float32),
            jax.ShapeDtypeStruct((2, width, LANES), jnp.float32),
            jax.ShapeDtypeStruct((n, cols) + piece.shape, jnp.float32),
        ],
        scratch_shapes=[
            pltpu.VMEM(gate.shape, jnp.bfloat16),
            pltpu.VMEM(gate.shape, jnp.bfloat16),
            pltpu.VMEM(low.shape, jnp.bfloat16),
            pltpu.VMEM(high.shape, jnp.bfloat16),
            pltpu.VMEM((3, 2, lines, LANES), jnp.float32),
            pltpu.VMEM((3, 2, lines, LANES), jnp.float32),
            dma(7, count), dma(7, count), dma(8),
            dma(3), dma(3), dma(3), dma(3), dma(cols), dma(cols),
        ],
        compiler_params=pltpu.CompilerParams(collective_id=0, has_side_effects=True),
    )(gate, up, low, high, piece)


def shards(mesh, train_gate, low_gate, high_gate, train_up, low_up, high_up, norm_train, norm_step):
    low = jnp.concatenate([low_gate.T, low_up.T], axis=0)
    high = jnp.concatenate([high_gate, high_up], axis=0).T
    all_gate, all_up, all_low, total, scale, all_norm = gathered(
        mesh, train_gate.T, train_up.T, low, high, norm_train + norm_step
    )
    ready_gate, ready_up = merge(all_gate, all_up, all_low, high, scale)
    width = high.shape[0]
    full, rest = divmod(width, LANES)
    sums = total[:, :full].reshape(2, -1)
    if rest:
        sums = jnp.concatenate([sums, total[:, full, LANES - rest:]], axis=1)
    factors = sums / ready_gate.shape[1]
    serve_norm = all_norm[:, :, 0, :].reshape(-1).astype(jnp.bfloat16)
    return ready_gate.T, ready_up.T, factors[0], factors[1], serve_norm


def shards_any(mesh, train_gate, low_gate, high_gate, train_up, low_up, high_up, norm_train, norm_step):
    def sums(train, low, high):
        latest = train.astype(jnp.float32) + mix_rate * jnp.dot(low, high, preferred_element_type=jnp.float32)
        return jnp.sum(jnp.abs(latest), axis=0)

    gather = lambda a: lax.all_gather(a, "zero", axis=0)
    low = jnp.concatenate([low_gate.T, low_up.T], axis=0)
    high = jnp.concatenate([high_gate, high_up], axis=0).T
    all_gate, all_up, all_low = gather(train_gate.T), gather(train_up.T), gather(low)
    total = lax.psum(jnp.stack([sums(train_gate, low_gate, high_gate), sums(train_up, low_up, high_up)]), "zero")
    factors = total / (mesh.shape["zero"] * train_gate.shape[0])
    scale = jnp.broadcast_to((1.0 / factors)[:, :, None], factors.shape + (LANES,))
    ready_gate, ready_up = merge(all_gate, all_up, all_low, high, scale)
    serve_norm = lax.all_gather(
        (norm_train + norm_step).astype(jnp.bfloat16), ("zero", "cols"), axis=0, tiled=True
    )
    return ready_gate.T, ready_up.T, factors[0], factors[1], serve_norm


def solution(mesh):
    body = shards if mesh.shape["zero"] == 1 << 3 else shards_any
    return jax.shard_map(
        functools.partial(body, mesh),
        mesh=mesh,
        in_specs=(
            P("zero", "cols"),
            P("zero", None),
            P(None, "cols"),
            P("zero", "cols"),
            P("zero", None),
            P(None, "cols"),
            P(("zero", "cols")),
            P(("zero", "cols")),
        ),
        out_specs=(P(None, "cols"), P(None, "cols"), P("cols"), P("cols"), P()),
        check_vma=False,
    )
```

time: 324 us -> 262 us (0.81)
  Pallas kernels: 0 us -> 248 us
  waiting for transfers between devices: 168 us -> 0 us
  blocking collectives: 91.5 us -> 0 us
  local copies, waits for them, and re-layouts: 31.3 us -> 8.62 us
  between operations: 14.1 us -> 0.68 us
  matrix products: 8.98 us -> 0 us
  other arithmetic: 9.46 us -> 3.47 us
    pallas_call x0 -> x2, Pallas kernels: none -> 248 us  [the longest x1 205 us: gathered(): pl.pallas_call(functools.partial(gather_kernel, n, cols, ('zero', 'cols')...]
    all_gather x2 -> x0, waiting for transfers between devices: 168 us -> none  [the longest x1 121 us: shards(): lax.all_gather(narrow_gate, 'zero', axis=0, tiled=True)]
    all_gather x1 -> x0, blocking collectives: 66 us -> none  [shards(): lax.all_gather((norm_train + norm_step).astype(jnp.bfloat16), ('zero', 'c...]
    unnamed x22 -> x12, local copies, waits for them, and re-layouts: 31.3 us -> 5.75 us
    psum x1 -> x0, blocking collectives: 25.5 us -> none  [shards(): lax.psum((jnp.sum(jnp.abs(latest_gate), axis=0), jnp.sum(jnp.abs(latest_u...]
    dot_general x2 -> x0, matrix products: 8.98 us -> none  [the longest x1 5.44 us: shards(): jnp.dot(low_gate, high_gate, preferred_element_type=jnp.float32)]
    convert_element_type x2 -> x0, other arithmetic: 8.8 us -> none  [the longest x1 4.42 us: shards(): (latest_up / factor_up).astype(jnp.bfloat16)]
  transfers between devices with their start and end apart: 2 -> 0, of which waited for: 2 -> 0; matrix products, arithmetic and copies ran while one was open for 2% -> 0% of each run, Pallas kernels for 0% -> 0%
where the time goes in v1:
time: 262 us; the launch traced here: 261 us
  Pallas kernels  248 us (95%)
  local copies, waits for them, and re-layouts  8.62 us (3%)
  other arithmetic  3.47 us (1%)
    pallas_call x1, Pallas kernels, gathered(): pl.pallas_call(functools.partial(gather_kernel, n, cols, ('zero', 'cols')...  205 us
    pallas_call x1, Pallas kernels, merge(): pl.pallas_call(merge_kernel, grid=(width // block, n), in_specs=[shard, s...  43.3 us
    unnamed x12, local copies, waits for them, and re-layouts  5.75 us

profile of v1, /device:TPU:0, one launch (start us, length us, event | category | flops | bytes accessed | tf_op | source)
XLA Modules:
  0.0 261.2 jit_solution(16245393453376273553)
XLA Ops:
  0.6 0.7 add.3
  1.3 0.6 broadcast_in_dim.2.norm
  1.9 1.5 pad_maximum_fusion.low
  3.4 1.4 copy.15
  4.8 1.4 copy.16
  6.1 1.2 maximum_bitcast_fusion.high
  7.4 0.0 copy-start
  7.4 205.2 %shard_map.119 = (bf16[8,2752,512]{2,1,0:T(8,128)(2,1)}, bf16[8,2752,512]{2,1,0:T(8,128)(2,1)}, bf16[8,128,512]{2,1,0:T(8,128)(2,1)}, f32[2,22,128]{2,1,0:T(8,12...) custom-call(bf16[2752,512]{1,0:T(8,128)(2,1)} %bitcast.15, bf16[2752,512]{1,0:T(8,128)(2,1)} %bitcast.16, ...), custom_call_target="tpu_custom_call" | custom-call | tf_op jit(solution)/shard_map/pallas_call | solution.py:266
  212.6 0.0 copy-done
  212.6 0.0 copy-start.1
  212.6 1.8 copy-done.1
  214.4 0.0 copy-start.2
  214.4 1.2 copy-done.2
  215.6 0.0 copy-start.3
  215.6 43.3 %shard_map.120 = (bf16[2752,4096]{1,0:T(8,128)(2,1)}, bf16[2752,4096]{1,0:T(8,128)(2,1)}) custom-call(bf16[8,2752,512]{2,1,0:T(8,128)(2,1)} %get-tuple-element.13.gate, bf16[8,2752,512]{2,1,0:T(8,128)(2,1)} %get-tuple-element.14.up, bf16[8,128,512]{2,1,0:T(8,128)(2,1)S(1)} %copy-done.2, bf16[2752,128]{1,0:T(8,128)(2,1)S(1)} %copy-done, ...), custom_call_target="tpu_custom_call" | custom-call | tf_op jit(solution)/shard_map/pallas_call | solution.py:241
  258.9 0.0 copy-done.3
  258.9 0.1 slice.17
  259.0 0.7 slice_reduce_fusion
  259.6 1.5 fusion
  (3 shorter events, 0.0 us)
Async XLA Ops:
  7.4 205.2 %copy-start = (bf16[2752,128]{1,0:T(8,128)(2,1)S(1)}, bf16[2752,128]{1,0:T(8,128)(2,1)}, u32[]{:S(2)}) copy-start(bf16[2752,128]{1,0:T(8,128)(2,1)} %maximum_bitcast_fusion.high) | copy-start | bytes 2113540
  212.6 1.8 copy-start.1
  214.4 1.2 copy-start.2
  215.6 43.3 %copy-start.3 = (f32[2,22,128]{2,1,0:T(8,128)S(1)}, f32[2,22,128]{2,1,0:T(8,128)}, u32[]{:S(2)}) copy-start(f32[2,22,128]{2,1,0:T(8,128)} %get-tuple-element.19) | copy-start | bytes 67588
